TPU v7x, 128 devices: a whole 4x4x4 slice. The times are simulated.
128 devices in a mesh: task: 8 (over x_hi, y), tp: 16 (over z, x_lo, core).
Axes of the slice: x: 4 (x_hi: 2, x_lo: 2; x = x_hi * 2 + x_lo), y: 4, z: 4, core: 2. Of those that a mesh axis runs over, the one named last changes fastest.
Arguments:
- observations: bfloat16 [256, 16, 4096], P('task', None, 'tp'), may hold values from -6 to 6
- gain: float32 [4096], P('tp'), may hold values from 0.5 to 1.5
- w_in: bfloat16 [4096, 4096], P(None, 'tp'), may hold values from -0.09375 to 0.09375
- w_mix: bfloat16 [4096, 4096], P('tp'), may hold values from -0.09375 to 0.09375
- w_out: bfloat16 [4096, 4096], P(None, 'tp'), may hold values from -0.09375 to 0.09375
- w_head: bfloat16 [4096, 75], P('tp'), may hold values from -0.09375 to 0.09375
- head_bias: float32 [75], replicated, may hold values from -4 to 4
- pop_mean: float32 [57], replicated, may hold values from -8 to 8
- pop_scale: float32 [57], replicated, may hold values from 0.5 to 4
- task_indices: int32 [256], P('task'), may hold values from 0 to 56
- actions: int32 [256, 15], P('task'), may hold values from 0 to 17
- rewards: float32 [256, 15], P('task'), may hold values from -18 to 27
- episode_ends: int32 [256, 15], P('task'), may hold values 0 or 1
- behaviour_log_prob: float32 [256, 15], P('task'), may hold values from -4.5 to -1.5
Outputs:
- grad_w_in: float32 [4096, 4096], P(None, 'tp')
- grad_w_mix: float32 [4096, 4096], P('tp')
- grad_w_out: float32 [4096, 4096], P(None, 'tp')
- grad_gain: float32 [4096], P('tp')
- grad_head: float32 [4096, 75], P('tp')
- grad_head_bias: float32 [75], replicated
- new_head: bfloat16 [4096, 75], P('tp')
- new_bias: float32 [75], replicated
- updated_return_mean: float32 [57], replicated
- updated_return_scale: float32 [57], replicated
All inputs are finite; a program needn't handle non-finite values. No bound on the sum of `episode_ends` on one device may be relied on, other than what follows from the above.
Results may differ from a plain program's by a relative error of at most 0.03.
Values may be sent and summed in bfloat16 or wider, within the bound.
A program may use at most 128 MiB of HBM per device.

v0:
```python
import jax
import jax.numpy as jnp
from jax import lax
from jax.sharding import PartitionSpec as P

ACTIONS = 18
TASKS = 57
DISCOUNT = 0.99
BASELINE_COST = 0.5
ENTROPY_COST = 0.01
POPART_PRIOR = 64.0
NORM_EPS = 1e-06


def sent_to_all(value, axis):
    copies = jnp.broadcast_to(value, (lax.axis_size(axis), *value.shape))
    return lax.all_to_all(copies, axis, split_axis=0, concat_axis=0, tiled=True)


def of_everyone(value, axis):
    everything = sent_to_all(value, axis)
    return jnp.sum(everything, axis=0)


def packed_total(arrays, axis):
    line, at, gathered = (jnp.concatenate([a.reshape(-1) for a in arrays]), 0, [])
    subtotal = of_everyone(line, axis)
    for a in arrays:
        gathered.append(subtotal[at : at + a.size].reshape(a.shape))
        at += a.size
    return tuple(gathered)


def cut_along(value, dim, devices):
    before, after = (value.shape[:dim], value.shape[dim + 1 :])
    return jnp.moveaxis(value.reshape(*before, devices, -1, *after), dim, 0)


def sum_at_owner(value, axis, dim):
    parts = cut_along(value, dim, lax.axis_size(axis))
    arrived = lax.all_to_all(parts, axis, split_axis=0, concat_axis=0, tiled=True)
    return arrived.astype(jnp.float32).sum(axis=0)


def joined_along(parts, dim):
    dims = list(parts.shape[1:])
    dims[dim] *= parts.shape[0]
    return jnp.moveaxis(parts, 0, dim).reshape(dims)


def gathered_copies(value, axis, dim):
    parts = sent_to_all(value, axis)
    return joined_along(parts, dim)


def summed_on_arrival(value, axis, dim):
    parts = cut_along(value, dim, lax.axis_size(axis))
    arrived = lax.all_to_all(parts, axis, split_axis=0, concat_axis=0, tiled=True)
    return arrived.sum(axis=0)


def silu_slope(before):
    sigmoid = jax.nn.sigmoid(before)
    return sigmoid * (1.0 + before * (1.0 - sigmoid))


def discounted_sums(values, factors):

    def advance(running, column):
        latest = column[0] + column[1] * running
        return (latest, latest)

    opening = jnp.zeros((values.shape[0],), jnp.float32)
    ending, stacked = lax.scan(advance, opening, (values.T, factors.T), reverse=True)
    return stacked.T


def task_onehot(task_indices):
    return (task_indices[:, None] == jnp.arange(TASKS, dtype=jnp.int32)[None, :]).astype(
        jnp.float32
    )


def popart_partials(task_indices, rewards, discount_factors):
    returns = discounted_sums(rewards, discount_factors)
    task_table = task_onehot(task_indices)
    counts = jnp.sum(task_table, axis=0) * rewards.shape[1]
    totals = jnp.dot(task_table.T, jnp.sum(returns, axis=1))
    squares = jnp.dot(task_table.T, jnp.sum(returns * returns, axis=1))
    return (counts, totals, squares)


def popart_update(counts, totals, squares, pop_mean, pop_scale):
    mixing = counts / (counts + POPART_PRIOR)
    safe_counts = jnp.maximum(counts, 1.0)
    batch_mean = totals / safe_counts
    batch_square = squares / safe_counts
    updated_return_mean = (1.0 - mixing) * pop_mean + mixing * batch_mean
    mean_gap = batch_mean - pop_mean
    variance = (
        (1.0 - mixing) * pop_scale * pop_scale
        + mixing * (batch_square - batch_mean * batch_mean)
        + mixing * (1.0 - mixing) * mean_gap * mean_gap
    )
    return (updated_return_mean, jnp.sqrt(variance))


def rescale_head(w_head, head_bias, pop_mean, pop_scale, updated_return_mean, updated_return_scale):
    scale_ratio = pop_scale / updated_return_scale
    column_scale = jnp.concatenate([jnp.ones((ACTIONS,), jnp.float32), scale_ratio])
    new_head = (w_head.astype(jnp.float32) * column_scale[None, :]).astype(jnp.bfloat16)
    value_bias = (
        pop_scale * head_bias[ACTIONS:] + pop_mean - updated_return_mean
    ) / updated_return_scale
    new_bias = jnp.concatenate([head_bias[:ACTIONS], value_bias])
    return (new_head, new_bias)


def importance_trace_loss(
    head_value_estimates,
    task_indices,
    actions,
    rewards,
    discount_factors,
    behaviour_log_prob,
    updated_return_mean,
    updated_return_scale,
    loss_weighting,
):
    task_table = task_onehot(task_indices)
    env_mean = jnp.dot(task_table, updated_return_mean)[:, None]
    env_scale = jnp.dot(task_table, updated_return_scale)[:, None]
    logits = head_value_estimates[:, :-1, :ACTIONS]
    norm_values = jnp.sum(head_value_estimates[:, :, ACTIONS:] * task_table[:, None, :], axis=2)
    values = lax.stop_gradient(norm_values * env_scale + env_mean)
    log_total = jnp.log(jnp.sum(jnp.exp(logits), axis=2))
    chosen = actions[:, :, None] == jnp.arange(ACTIONS, dtype=jnp.int32)[None, None, :]
    log_policy = jnp.sum(jnp.where(chosen, logits, 0.0), axis=2) - log_total
    clipped = jnp.minimum(jnp.exp(lax.stop_gradient(log_policy) - behaviour_log_prob), 1.0)
    deltas = clipped * (rewards + discount_factors * values[:, 1:] - values[:, :-1])
    targets = values[:, :-1] + discounted_sums(deltas, discount_factors * clipped)
    following = jnp.concatenate([targets[:, 1:], values[:, -1:]], axis=1)
    advantage = lax.stop_gradient(
        clipped
        * ((rewards + discount_factors * following - env_mean) / env_scale - norm_values[:, :-1])
    )
    normed_targets = lax.stop_gradient((targets - env_mean) / env_scale)
    policy = jnp.exp(logits - log_total[:, :, None])
    entropy = -jnp.sum(policy * (logits - log_total[:, :, None]), axis=2)
    per_frame = (
        -advantage * log_policy
        + 0.5 * BASELINE_COST * (normed_targets - norm_values[:, :-1]) ** 2
        - ENTROPY_COST * entropy
    )
    return loss_weighting * jnp.sum(per_frame)


def on_device(
    observations,
    gain,
    w_in,
    w_mix,
    w_out,
    w_head,
    head_bias,
    pop_mean,
    pop_scale,
    task_indices,
    actions,
    rewards,
    episode_ends,
    behaviour_log_prob,
):
    env_count, frames, part_width = observations.shape
    groups = lax.axis_size("tp")
    full_width = part_width * groups
    row_count = env_count * frames
    local_rows = row_count // groups
    own_tokens = observations.reshape(row_count, part_width)
    discount_factors = DISCOUNT * (1.0 - episode_ends.astype(jnp.float32))
    counts, totals, squares = popart_partials(task_indices, rewards, discount_factors)
    counts, totals, squares = packed_total((counts, totals, squares), "task")
    updated_return_mean, updated_return_scale = popart_update(
        counts, totals, squares, pop_mean, pop_scale
    )
    new_head, new_bias = rescale_head(
        w_head, head_bias, pop_mean, pop_scale, updated_return_mean, updated_return_scale
    )
    loss_weighting = float(env_count * lax.axis_size("task")) ** (-0.5)
    tokens, gain_all = (
        lax.all_gather(own_tokens, "tp", axis=1, tiled=True),
        lax.all_gather(gain.astype(jnp.bfloat16), "tp", axis=0, tiled=True).astype(gain.dtype),
    )
    row_offset = lax.axis_index("tp") * local_rows
    token_rows = lax.dynamic_slice_in_dim(tokens, row_offset, local_rows, 0)
    pre_in = jnp.dot(tokens, w_in, preferred_element_type=jnp.float32)
    hidden_in = jax.nn.silu(pre_in).astype(jnp.bfloat16)
    hidden_rows = hidden_in
    mix_sum = lax.psum_scatter(
        jnp.dot(hidden_rows, w_mix, preferred_element_type=jnp.float32).astype(jnp.bfloat16),
        "tp",
        scatter_dimension=0,
        tiled=True,
    ).astype(jnp.float32)
    residual = token_rows.astype(jnp.float32) + mix_sum
    inverse = lax.rsqrt(jnp.mean(residual * residual, axis=1, keepdims=True) + NORM_EPS)
    normed = (residual * inverse * gain_all[None, :]).astype(jnp.bfloat16)
    normed_all = lax.all_gather(normed, "tp", axis=0, tiled=True)
    pre_out = jnp.dot(normed_all, w_out, preferred_element_type=jnp.float32)
    hidden_out = jax.nn.silu(pre_out).astype(jnp.bfloat16)
    head_terms = jnp.dot(hidden_out, new_head, preferred_element_type=jnp.float32)
    env_share = env_count // groups
    env_offset = lax.axis_index("tp") * env_share

    def select_envs(source):
        return lax.dynamic_slice_in_dim(source, env_offset, env_share, 0)

    head_value_estimates = (
        sum_at_owner(head_terms.astype(jnp.bfloat16), "tp", 0) + new_bias[None, :]
    )
    head_value_estimates = head_value_estimates.reshape(env_share, frames, -1)

    def share_loss(network_outputs):
        return importance_trace_loss(
            network_outputs,
            select_envs(task_indices),
            select_envs(actions),
            select_envs(rewards),
            select_envs(discount_factors),
            select_envs(behaviour_log_prob),
            updated_return_mean,
            updated_return_scale,
            loss_weighting,
        )

    loss_value, pullback = jax.vjp(share_loss, head_value_estimates)
    (d_heads,) = pullback(jnp.ones((), jnp.float32))
    d_local = d_heads.reshape(env_share * frames, -1).astype(jnp.bfloat16)
    d_rounded = gathered_copies(d_local, "tp", 0)
    grad_head = jnp.dot(hidden_out.T, d_rounded, preferred_element_type=jnp.float32)
    grad_bias = jnp.sum(d_rounded.astype(jnp.float32), axis=0)
    d_hidden_out = jnp.dot(d_rounded, new_head.T, preferred_element_type=jnp.float32)
    d_pre_out = (d_hidden_out * silu_slope(pre_out)).astype(jnp.bfloat16)
    grad_out = jnp.dot(normed_all.T, d_pre_out, preferred_element_type=jnp.float32)
    d_normed = lax.psum_scatter(
        jnp.dot(d_pre_out, w_out.T, preferred_element_type=jnp.float32).astype(jnp.bfloat16),
        "tp",
        scatter_dimension=0,
        tiled=True,
    ).astype(jnp.float32)
    scaled = d_normed * gain_all[None, :]
    inner_sum = jnp.sum(scaled * residual, axis=1, keepdims=True)
    d_residual = (inverse * scaled - residual * inverse**3 * inner_sum / full_width).astype(
        jnp.bfloat16
    )
    grad_gain = summed_on_arrival(jnp.sum(d_normed * residual * inverse, axis=0), "tp", 0)
    arrived = lax.all_gather(d_residual, "tp", axis=0, tiled=True)
    hidden_rows = hidden_in
    grad_part = jnp.dot(hidden_rows.T, arrived, preferred_element_type=jnp.float32)
    d_hidden = jnp.dot(arrived, w_mix.T, preferred_element_type=jnp.float32)
    grad_mix = grad_part
    d_pre_in = (d_hidden * silu_slope(pre_in)).astype(jnp.bfloat16)
    grad_in = jnp.dot(tokens.T, d_pre_in, preferred_element_type=jnp.float32)
    grad_in, grad_mix, grad_out, grad_gain, grad_head, grad_bias = (
        lax.psum(grad_in.astype(jnp.bfloat16), "task").astype(jnp.float32),
        lax.psum(grad_mix.astype(jnp.bfloat16), "task").astype(jnp.float32),
        lax.psum(grad_out.astype(jnp.bfloat16), "task").astype(jnp.float32),
        lax.psum(grad_gain.astype(jnp.bfloat16), "task").astype(jnp.float32),
        lax.psum(grad_head.astype(jnp.bfloat16), "task").astype(jnp.float32),
        lax.psum(grad_bias.astype(jnp.bfloat16), "task").astype(jnp.float32),
    )
    return (
        grad_in,
        grad_mix,
        grad_out,
        grad_gain,
        grad_head,
        grad_bias,
        new_head,
        new_bias,
        updated_return_mean,
        updated_return_scale,
    )


def solution(mesh):
    in_specs = (
        P("task", None, "tp"),
        P("tp"),
        P(None, "tp"),
        P("tp", None),
        P(None, "tp"),
        P("tp", None),
        P(),
        P(),
        P(),
        P("task"),
        P("task", None),
        P("task", None),
        P("task", None),
        P("task", None),
    )
    out_specs = (
        P(None, "tp"),
        P("tp", None),
        P(None, "tp"),
        P("tp"),
        P("tp", None),
        P(),
        P("tp", None),
        P(),
        P(),
        P(),
    )
    return jax.shard_map(
        on_device, mesh=mesh, in_specs=in_specs, out_specs=out_specs, check_vma=False
    )
```

profile of v0, /device:TPU:1, one launch (start us, length us, event | category | flops | bytes accessed | tf_op | source)
XLA Modules:
  0.0 498.5 jit_solution(18199204609391938755)
XLA Ops:
  7.2 0.7 all-gather.5.cloned.1.call-update
  8.0 50.4 %all-gather.5.cloned.1.call-done = bf16[512,4096]{1,0:T(8,128)(2,1)} async-done(((bf16[512,256]{1,0:T(8,128)(2,1)}), bf16[512,4096]{1,0:T(8,128)(2,1)}) %all-gather.5.cloned.1.call-update) | async-done | bytes 4194320 | tf_op jit(solution)/shard_map/all_gather | solution.py:191
  58.4 4.1 fusion.46
  62.5 3.3 convolution_convert_fusion.1
  66.0 18.6 %all-gather = bf16[16,1,256]{2,1,0:T(2,128)(2,1)S(1)} all-gather(bf16[1,1,256]{2,1,0:T(2,128)(2,1)S(1)} %reshape.98), channel_id=1, replica_groups=mesh['task'=8,'tp'=16] {'tp'}, dimensions={0}, use_global_device_ids=true | all-gather | bytes 8704 | tf_op jit(solution)/shard_map/all_gather | solution.py:192
  84.6 49.5 %reduce-scatter.3.cloned.1.call-done = bf16[32,4096]{1,0:T(8,128)(2,1)} async-done(((bf16[512,4096]{1,0:T(8,128)(2,1)}), bf16[32,4096]{1,0:T(8,128)(2,1)}) %reduce-scatter.3.cloned.1.call-update) | async-done | bytes 262160 | tf_op jit(solution)/shard_map/reduce_scatter | solution.py:199
  134.1 1.2 multiply_reduce_fusion
  135.3 0.5 multiply_multiply_fusion.1
  135.8 1.8 multiply_convert_fusion.1
  137.7 0.1 copy.85
  137.8 0.1 copy.86
  137.9 1.1 while.34
  139.1 0.1 convolution_bitcast_fusion.3
  139.2 0.1 convolution_bitcast_fusion.2
  139.3 0.1 convert_reduce_fusion.1
  139.5 0.6 broadcast_in_dim.72
  140.1 6.2 %all-to-all-start = ((f32[8,1,171]{2,1,0:T(1,128)}), f32[8,1,171]{2,1,0:T(1,128)S(1)}, u32[]{:S(2)}, u32[]{:S(2)}) async-start(f32[8,1,171]{2,1,0:T(1,128)} %broadcast_in_dim.72), calls=%async_computation.1 | async-start | bytes 16384 | tf_op jit(solution)/shard_map/all_to_all | solution.py:17
  146.6 0.1 copy.89
  146.7 0.1 copy.116
  146.8 0.1 copy.115
  146.9 6.0 %all-to-all-done = f32[8,1,171]{2,1,0:T(1,128)S(1)} async-done(((f32[8,1,171]{2,1,0:T(1,128)}), f32[8,1,171]{2,1,0:T(1,128)S(1)}, u32[]{:S(2)}, u32[]{:S(2)}) %all-to-all-start) | async-done | bytes 5504 | tf_op jit(solution)/shard_map/all_to_all | solution.py:17
  152.9 0.1 subtract_divide_fusion
  153.1 0.2 convolution_bitcast_fusion.1
  153.3 0.2 convolution_bitcast_fusion
  153.5 0.1 multiply_convert_fusion.3
  153.6 23.3 %all-gather.7.cloned.1.call-done = bf16[512,4096]{1,0:T(8,128)(2,1)} async-done(((bf16[32,4096]{1,0:T(8,128)(2,1)}), bf16[512,4096]{1,0:T(8,128)(2,1)}) %all-gather.7.cloned.1.call-update) | async-done | bytes 4194320 | tf_op jit(solution)/shard_map/all_gather | solution.py:208
  176.8 4.9 multiply_convert_fusion
  181.8 0.2 convolution_convert_fusion.5
  182.0 0.8 copy.88
  182.8 4.2 all-to-all-start.1
  187.0 6.0 %all-to-all-done.1 = bf16[16,32,75]{2,1,0:T(8,128)(2,1)S(1)} async-done(((bf16[16,32,75]{2,1,0:T(8,128)(2,1)}), bf16[16,32,75]{2,1,0:T(8,128)(2,1)S(1)}, u32[]{:S(2)}, u32[]{:S(2)}) %all-to-all-start.1) | async-done | bytes 76832 | tf_op jit(solution)/shard_map/all_to_all | solution.py:41
  193.1 0.1 exponential_reduce_fusion
  193.2 0.2 fusion.19
  193.5 0.2 multiply_reduce_fusion.1
  193.7 0.1 multiply_bitcast_fusion.1
  193.8 0.1 copy.96
  193.9 0.1 copy.97
  194.0 1.1 while.35
  195.1 0.1 copy.98
  195.4 0.1 add_divide_fusion.3
  195.5 0.1 multiply_add_fusion
  195.7 9.4 %all_to_all.25 = bf16[16,32,75]{2,1,0:T(8,128)(2,1)S(1)} all-to-all(bf16[16,32,75]{2,1,0:T(8,128)(2,1)S(1)} %broadcast_in_dim.79), channel_id=1, replica_groups=mesh['task'=8,'tp'=16] {'tp'}, dimensions={0} | all-to-all | bytes 153600 | tf_op jit(solution)/shard_map/all_to_all | solution.py:17
  205.1 1.3 fusion.5
  206.4 3.3 convolution_convert_fusion
  209.8 67.0 %reduce-scatter.5.cloned.1.call-done = bf16[32,4096]{1,0:T(8,128)(2,1)} async-done(((bf16[512,4096]{1,0:T(8,128)(2,1)}), bf16[32,4096]{1,0:T(8,128)(2,1)}) %reduce-scatter.5.cloned.1.call-update) | async-done | bytes 262160 | tf_op jit(solution)/shard_map/reduce_scatter | solution.py:245
  276.8 1.8 fusion.13
  278.7 2.0 fusion.10
  280.6 0.2 all-reduce.8.cloned.1.call-start
  280.9 4.8 convolution_convert_fusion.2
  285.7 33.9 %all-gather.9.cloned.1.call-done = bf16[512,4096]{1,0:T(8,128)(2,1)} async-done(((bf16[32,4096]{1,0:T(8,128)(2,1)}), bf16[512,4096]{1,0:T(8,128)(2,1)}) %all-gather.9.cloned.1.call-update) | async-done | bytes 4194320 | tf_op jit(solution)/shard_map/all_gather | solution.py:257
  319.6 9.4 %fusion.4 = bf16[4096,256]{0,1:T(8,128)(2,1)} fusion(bf16[512,4096]{1,0:T(8,128)(2,1)} %all-gather.5.cloned.1.call-done, bf16[512,4096]{1,0:T(8,128)(2,1)} %all-gather.9.cloned.1.call-done, bf16[256,4096]{1,0:T(8,128)(2,1)S(1)} %copy-done, f32[512,256]{1,0:T(8,128)S(1)} %fusion.46), kind=kOutput, calls=%fused_computation.11 | convolution fusion | flops 2149711872 | bytes 13107200 | tf_op jit(solution)/shard_map/dot_general | solution.py:263
  329.0 4.8 convolution_convert_fusion.3
  333.8 4.4 all-to-all-start.3
  338.2 0.2 convolution_convert_fusion.6
  338.4 0.1 reduce_sum.163
  338.5 5.5 %all-to-all-done.3 = f32[16,1,256]{2,1,0:T(1,128)S(1)} async-done(((f32[16,1,256]{2,1,0:T(1,128)}), f32[16,1,256]{2,1,0:T(1,128)S(1)}, u32[]{:S(2)}, u32[]{:S(2)}) %all-to-all-start.3) | async-done | bytes 16416 | tf_op jit(solution)/shard_map/all_to_all | solution.py:58
  344.0 38.7 %all-reduce.4 = (bf16[256]{0:T(256)(128)(2,1)S(1)}, bf16[256,75]{0,1:T(8,128)(2,1)S(1)}, bf16[75]{0:T(256)(128)(2,1)S(1)}) all-reduce(bf16[256]{0:T(256)(128)(2,1)S(1)} %reduce_sum.162, bf16[256,75]{0,1:T(8,128)(2,1)S(1)} %convolution_convert_fusion.6, bf16[75]{0:T(256)(128)(2,1)S(1)} %reduce_sum.163), channel_id=1, replica_groups=mesh['task'=8,'tp'=16] {'task'}, use_global_device_ids=true, to_apply=%region_23.24 | all-reduce | flops 19531 | bytes 78124 | tf_op jit(solution)/shard_map/psum | solution.py:268
  382.7 0.6 convert_element_type.138
  383.3 0.5 convert_element_type.141
  383.8 0.6 convert_element_type.140
  384.4 96.4 %all-reduce.8.cloned.1.call-done = (bf16[4096,256]{0,1:T(8,128)(2,1)}, bf16[256,4096]{1,0:T(8,128)(2,1)}, bf16[4096,256]{1,0:T(8,128)(2,1)}) async-done(((bf16[4096,256]{0,1:T(8,128)(2,1)}, bf16[256,4096]{1,0:T(8,128)(2,1)}, bf16[4096,256]{1,0:T(8,128)(2,1)}), (bf16[4096,256]{0,1:T(8,128)(2,1)}, bf16[256,4096]{1,0:T(8,128)(2,1)}, bf16[4096,256]{1,0:T(8,128)(2,1)})) %all-reduce.8.cloned.1.call-update) | async-done | bytes 6291472 | tf_op jit(solution)/shard_map/psum | solution.py:265
  480.8 4.3 copy.105
  485.1 4.2 convert_element_type.134
  489.3 2.3 convert_element_type.136
  (140 shorter events, 3.3 us)
Async XLA Ops:
  7.2 55.3 %copy-start = (bf16[256,4096]{1,0:T(8,128)(2,1)S(1)}, bf16[256,4096]{1,0:T(8,128)(2,1)}, u32[]{:S(2)}) copy-start(bf16[256,4096]{1,0:T(8,128)(2,1)} %param.21) | copy-start | bytes 6291460
  7.2 51.2 %all-gather.5.cloned.1.call-start = ((), (), s32[]{:S(2)}) async-start(), calls=%async_computation.6 | async-start | bytes 4456448 | tf_op jit(solution)/shard_map/all_gather | solution.py:191
  7.9 126.2 %reduce-scatter.3.cloned.1.call-start = ((), (), s32[]{:S(2)}) async-start(), calls=%async_computation.7 | async-start | bytes 4456448 | tf_op jit(solution)/shard_map/reduce_scatter | solution.py:199
  62.5 3.5 copy-start.17
  65.8 71.9 %copy-start.7 = (s32[32,15]{0,1:T(8,128)S(1)}, s32[32,15]{0,1:T(8,128)}, u32[]{:S(2)}) copy-start(s32[32,15]{0,1:T(8,128)} %param.30) | copy-start | bytes 5764
  65.8 72.1 %copy-start.6 = (f32[32,15]{0,1:T(8,128)S(1)}, f32[32,15]{0,1:T(8,128)}, u32[]{:S(2)}) copy-start(f32[32,15]{0,1:T(8,128)} %param.29) | copy-start | bytes 5764
  65.8 73.3 %copy-start.18 = (s32[32]{0:T(128)S(1)}, s32[32]{0:T(128)}, u32[]{:S(2)}) copy-start(s32[32]{0:T(128)} %param.27) | copy-start | bytes 388
  65.8 80.6 %copy-start.9 = (f32[32,15]{0,1:T(8,128)S(1)}, f32[32,15]{0,1:T(8,128)}, u32[]{:S(2)}) copy-start(f32[32,15]{0,1:T(8,128)} %param.31) | copy-start | bytes 5764
  65.8 80.7 %copy-start.8 = (s32[32,15]{0,1:T(8,128)S(1)}, s32[32,15]{0,1:T(8,128)}, u32[]{:S(2)}) copy-start(s32[32,15]{0,1:T(8,128)} %param.28) | copy-start | bytes 5764
  65.8 87.1 %copy-start.12 = (f32[57]{0:T(128)S(1)}, f32[57]{0:T(128)}, u32[]{:S(2)}) copy-start(f32[57]{0:T(128)} %param.25) | copy-start | bytes 688
  65.8 87.1 %copy-start.13 = (f32[57]{0:T(128)S(1)}, f32[57]{0:T(128)}, u32[]{:S(2)}) copy-start(f32[57]{0:T(128)} %param.26) | copy-start | bytes 688
  65.8 87.0 %copy-start.14 = (f32[75]{0:T(128)S(1)}, f32[75]{0:T(128)}, u32[]{:S(2)}) copy-start(f32[75]{0:T(128)} %param.24) | copy-start | bytes 904
  65.9 87.6 %copy-start.5 = (bf16[256,75]{0,1:T(8,128)(2,1)S(1)}, bf16[256,75]{0,1:T(8,128)(2,1)}, u32[]{:S(2)}) copy-start(bf16[256,75]{0,1:T(8,128)(2,1)} %param.23) | copy-start | bytes 115204
  65.9 111.0 %all-gather.7.cloned.1.call-start = ((), (), s32[]{:S(2)}) async-start(), calls=%async_computation.8 | async-start | bytes 4456448 | tf_op jit(solution)/shard_map/all_gather | solution.py:208
  135.8 1.9 copy-start.10
  140.1 12.7 %all-to-all-start = ((f32[8,1,171]{2,1,0:T(1,128)}), f32[8,1,171]{2,1,0:T(1,128)S(1)}, u32[]{:S(2)}, u32[]{:S(2)}) async-start(f32[8,1,171]{2,1,0:T(1,128)} %broadcast_in_dim.72), calls=%async_computation.1 | async-start | bytes 16384 | tf_op jit(solution)/shard_map/all_to_all | solution.py:17
  153.0 28.8 %copy-start.15 = (f32[57]{0:T(128)}, f32[57]{0:T(128)S(1)}, u32[]{:S(2)}) copy-start(f32[57]{0:T(128)S(1)} %get-tuple-element.394) | copy-start | bytes 688
  153.0 28.8 %copy-start.16 = (f32[57]{0:T(128)}, f32[57]{0:T(128)S(1)}, u32[]{:S(2)}) copy-start(f32[57]{0:T(128)S(1)} %get-tuple-element.395) | copy-start | bytes 688
  153.6 51.5 %copy-start.4 = (bf16[256,75]{0,1:T(8,128)(2,1)}, bf16[256,75]{0,1:T(8,128)(2,1)S(1)}, u32[]{:S(2)}) copy-start(bf16[256,75]{0,1:T(8,128)(2,1)S(1)} %multiply_convert_fusion.3) | copy-start | bytes 115204
  182.8 10.3 %all-to-all-start.1 = ((bf16[16,32,75]{2,1,0:T(8,128)(2,1)}), bf16[16,32,75]{2,1,0:T(8,128)(2,1)S(1)}, u32[]{:S(2)}, u32[]{:S(2)}) async-start(bf16[16,32,75]{2,1,0:T(8,128)(2,1)} %bitcast.8), calls=%async_computation.2 | async-start | bytes 262144 | tf_op jit(solution)/shard_map/all_to_all | solution.py:41
  186.9 89.9 %reduce-scatter.5.cloned.1.call-start = ((), (), s32[]{:S(2)}) async-start(), calls=%async_computation.9 | async-start | bytes 4456448 | tf_op jit(solution)/shard_map/reduce_scatter | solution.py:245
  187.0 6.0 %copy-start.11 = (f32[75]{0:T(128)}, f32[75]{0:T(128)S(1)}, u32[]{:S(2)}) copy-start(f32[75]{0:T(128)S(1)} %pad_maximum_fusion.1) | copy-start | bytes 904
  195.2 11.2 %copy-start.3 = (bf16[4096,256]{1,0:T(8,128)(2,1)S(1)}, bf16[4096,256]{1,0:T(8,128)(2,1)}, u32[]{:S(2)}) copy-start(bf16[4096,256]{1,0:T(8,128)(2,1)} %param.22) | copy-start | bytes 6291460
  209.7 67.1 %copy-start.1 = (bf16[32,4096]{1,0:T(8,128)(2,1)S(1)}, bf16[32,4096]{1,0:T(8,128)(2,1)}, u32[]{:S(2)}) copy-start(bf16[32,4096]{1,0:T(8,128)(2,1)} %reduce-scatter.3.cloned.1.call-done) | copy-start | bytes 786436
  209.7 109.8 %all-gather.9.cloned.1.call-start = ((), (), s32[]{:S(2)}) async-start(), calls=%async_computation.10 | async-start | bytes 4456448 | tf_op jit(solution)/shard_map/all_gather | solution.py:257
  280.6 200.2 %all-reduce.8.cloned.1.call-start = ((), (), s32[]{:S(2)}) async-start(), calls=%async_computation.11 | async-start | bytes 12582912 | tf_op jit(solution)/shard_map/psum | solution.py:265
  333.8 10.1 %all-to-all-start.3 = ((f32[16,1,256]{2,1,0:T(1,128)}), f32[16,1,256]{2,1,0:T(1,128)S(1)}, u32[]{:S(2)}, u32[]{:S(2)}) async-start(f32[16,1,256]{2,1,0:T(1,128)} %bitcast.20), calls=%async_computation.5 | async-start | bytes 32768 | tf_op jit(solution)/shard_map/all_to_all | solution.py:58
  485.1 4.3 copy-start.2
Sparse Core Ops, SparseCore 0:
  9.6 48.6 all-gather.4
  66.0 68.0 reduce-scatter.2
  137.8 38.9 all-gather.6
  209.9 66.9 reduce-scatter.4
  280.8 38.7 all-gather.8
  333.9 146.8 all-reduce.7
where the time goes:
time: 499 us
  waiting for transfers between devices  339 us (68%)
  blocking collectives  66.7 us (13%)
  matrix products  37 us (7%)
  other arithmetic  18 us (4%)
  starting transfers between devices  15.1 us (3%)
  between operations  14.4 us (3%)
  local copies, waits for them, and re-layouts  8.14 us (2%)
    psum x1, waiting for transfers between devices, on_device(): lax.psum(grad_in.astype(jnp.bfloat16), 'task').astype(jnp.float32)  96.4 us
    reduce_scatter x1, waiting for transfers between devices, on_device(): lax.psum_scatter(jnp.dot(d_pre_out, w_out.T, preferred_element_type=jnp.f...  67 us
    all_gather x1, waiting for transfers between devices, on_device(): lax.all_gather(own_tokens, 'tp', axis=1, tiled=True)  50.4 us
    reduce_scatter x1, waiting for transfers between devices, on_device(): lax.psum_scatter(jnp.dot(hidden_rows, w_mix, preferred_element_type=jnp.f...  49.5 us
    psum x1, blocking collectives, on_device(): lax.psum(grad_gain.astype(jnp.bfloat16), 'task').astype(jnp.float32)  38.7 us
    all_gather x1, waiting for transfers between devices, on_device(): arrived = lax.all_gather(d_residual, 'tp', axis=0, tiled=True)  33.9 us
    all_gather x1, waiting for transfers between devices, on_device(): normed_all = lax.all_gather(normed, 'tp', axis=0, tiled=True)  23.3 us
    all_gather x1, blocking collectives, on_device(): lax.all_gather(gain.astype(jnp.bfloat16), 'tp', axis=0, tiled=True)  18.6 us
  transfers between devices with their start and end apart: 9, of which 9 were waited for; matrix products, arithmetic and copies ran while one was open for 2% of the time, Pallas kernels for 0%

commit v1 on v0

--- a/solution.py
+++ b/solution.py
@@ -254,7 +254,9 @@
         jnp.bfloat16
     )
     grad_gain = summed_on_arrival(jnp.sum(d_normed * residual * inverse, axis=0), "tp", 0)
-    arrived = lax.all_gather(d_residual, "tp", axis=0, tiled=True)
+    arrived = jnp.concatenate(
+        lax.all_to_all(jnp.stack([d_residual] * lax.axis_size("tp")), "tp", 0, 0), axis=0
+    )
     hidden_rows = hidden_in
     grad_part = jnp.dot(hidden_rows.T, arrived, preferred_element_type=jnp.float32)
     d_hidden = jnp.dot(arrived, w_mix.T, preferred_element_type=jnp.float32)

time: 499 us -> 519 us (1.040)
  waiting for transfers between devices: 339 us -> 350 us
  starting transfers between devices: 15.1 us -> 22.1 us
    all_to_all x0 -> x1, waiting for transfers between devices: none -> 44.6 us  [on_device(): lax.all_to_all(jnp.stack([d_residual] * lax.axis_size('tp')), 'tp', 0, 0)]
    all_gather x1 -> x0, waiting for transfers between devices: 33.9 us -> none  [on_device(): arrived = lax.all_gather(d_residual, 'tp', axis=0, tiled=True)]
    all_to_all x0 -> x1, starting transfers between devices: none -> 7.16 us  [on_device(): lax.all_to_all(jnp.stack([d_residual] * lax.axis_size('tp')), 'tp', 0, 0)]
where the time goes in v1:
time: 519 us; the launch traced here: 518 us
  waiting for transfers between devices  350 us (67%)
  blocking collectives  66.7 us (13%)
  matrix products  37 us (7%)
  starting transfers between devices  22.1 us (4%)
  other arithmetic  17.3 us (3%)
  between operations  14.1 us (3%)
  local copies, waits for them, and re-layouts  10.7 us (2%)
    psum x1, waiting for transfers between devices, on_device(): lax.psum(grad_in.astype(jnp.bfloat16), 'task').astype(jnp.float32)  96.7 us
    reduce_scatter x1, waiting for transfers between devices, on_device(): lax.psum_scatter(jnp.dot(d_pre_out, w_out.T, preferred_element_type=jnp.f...  67.1 us
    all_gather x1, waiting for transfers between devices, on_device(): lax.all_gather(own_tokens, 'tp', axis=1, tiled=True)  50.4 us
    reduce_scatter x1, waiting for transfers between devices, on_device(): lax.psum_scatter(jnp.dot(hidden_rows, w_mix, preferred_element_type=jnp.f...  49.5 us
    all_to_all x1, waiting for transfers between devices, on_device(): lax.all_to_all(jnp.stack([d_residual] * lax.axis_size('tp')), 'tp', 0, 0)  44.6 us
    psum x1, blocking collectives, on_device(): lax.psum(grad_gain.astype(jnp.bfloat16), 'task').astype(jnp.float32)  38.7 us
    all_gather x1, waiting for transfers between devices, on_device(): normed_all = lax.all_gather(normed, 'tp', axis=0, tiled=True)  23.3 us
    all_gather x1, blocking collectives, on_device(): lax.all_gather(gain.astype(jnp.bfloat16), 'tp', axis=0, tiled=True)  18.6 us
  transfers between devices with their start and end apart: 9, of which 9 were waited for; matrix products, arithmetic and copies ran while one was open for 2% of the time, Pallas kernels for 0%

profile of v1, /device:TPU:1, one launch (start us, length us, event | category | flops | bytes accessed | tf_op | source)
XLA Modules:
  0.0 518.1 jit_solution(10609982780571305390)
XLA Ops:
  7.2 0.7 all-gather.4.cloned.1.call-update
  8.0 50.4 %all-gather.4.cloned.1.call-done = bf16[512,4096]{1,0:T(8,128)(2,1)} async-done(((bf16[512,256]{1,0:T(8,128)(2,1)}), bf16[512,4096]{1,0:T(8,128)(2,1)}) %all-gather.4.cloned.1.call-update) | async-done | bytes 4194320 | tf_op jit(solution)/shard_map/all_gather | solution.py:191
  58.4 4.1 fusion.46
  62.5 3.3 convolution_convert_fusion.1
  66.0 18.6 %all-gather = bf16[16,1,256]{2,1,0:T(2,128)(2,1)S(1)} all-gather(bf16[1,1,256]{2,1,0:T(2,128)(2,1)S(1)} %reshape.104), channel_id=1, replica_groups=mesh['task'=8,'tp'=16] {'tp'}, dimensions={0}, use_global_device_ids=true | all-gather | bytes 8704 | tf_op jit(solution)/shard_map/all_gather | solution.py:192
  84.6 49.5 %reduce-scatter.3.cloned.1.call-done = bf16[32,4096]{1,0:T(8,128)(2,1)} async-done(((bf16[512,4096]{1,0:T(8,128)(2,1)}), bf16[32,4096]{1,0:T(8,128)(2,1)}) %reduce-scatter.3.cloned.1.call-update) | async-done | bytes 262160 | tf_op jit(solution)/shard_map/reduce_scatter | solution.py:199
  134.1 1.2 multiply_reduce_fusion
  135.3 0.5 multiply_multiply_fusion.1
  135.8 1.8 multiply_convert_fusion.1
  137.7 0.1 copy.85
  137.8 0.1 copy.86
  137.9 1.1 while.34
  139.1 0.1 convolution_bitcast_fusion.3
  139.2 0.1 convolution_bitcast_fusion.2
  139.3 0.1 convert_reduce_fusion.1
  139.5 0.6 broadcast_in_dim.72
  140.1 6.2 %all-to-all-start = ((f32[8,1,171]{2,1,0:T(1,128)}), f32[8,1,171]{2,1,0:T(1,128)S(1)}, u32[]{:S(2)}, u32[]{:S(2)}) async-start(f32[8,1,171]{2,1,0:T(1,128)} %broadcast_in_dim.72), calls=%async_computation.1 | async-start | bytes 16384 | tf_op jit(solution)/shard_map/all_to_all | solution.py:17
  146.6 0.1 copy.89
  146.7 0.1 copy.116
  146.8 0.1 copy.115
  146.9 6.0 %all-to-all-done = f32[8,1,171]{2,1,0:T(1,128)S(1)} async-done(((f32[8,1,171]{2,1,0:T(1,128)}), f32[8,1,171]{2,1,0:T(1,128)S(1)}, u32[]{:S(2)}, u32[]{:S(2)}) %all-to-all-start) | async-done | bytes 5504 | tf_op jit(solution)/shard_map/all_to_all | solution.py:17
  152.9 0.1 subtract_divide_fusion
  153.1 0.2 convolution_bitcast_fusion.1
  153.3 0.2 convolution_bitcast_fusion
  153.6 23.3 %all-gather.6.cloned.1.call-done = bf16[512,4096]{1,0:T(8,128)(2,1)} async-done(((bf16[32,4096]{1,0:T(8,128)(2,1)}), bf16[512,4096]{1,0:T(8,128)(2,1)}) %all-gather.6.cloned.1.call-update) | async-done | bytes 4194320 | tf_op jit(solution)/shard_map/all_gather | solution.py:208
  176.8 4.9 multiply_convert_fusion
  181.8 0.2 convolution_convert_fusion.5
  182.0 0.8 copy.88
  182.8 4.2 all-to-all-start.1
  187.0 6.0 %all-to-all-done.1 = bf16[16,32,75]{2,1,0:T(8,128)(2,1)S(1)} async-done(((bf16[16,32,75]{2,1,0:T(8,128)(2,1)}), bf16[16,32,75]{2,1,0:T(8,128)(2,1)S(1)}, u32[]{:S(2)}, u32[]{:S(2)}) %all-to-all-start.1) | async-done | bytes 76832 | tf_op jit(solution)/shard_map/all_to_all | solution.py:41
  193.1 0.1 exponential_reduce_fusion
  193.2 0.2 fusion.19
  193.5 0.2 multiply_reduce_fusion.1
  193.8 0.1 copy.96
  193.9 0.1 copy.97
  194.0 1.1 while.35
  195.1 0.1 copy.98
  195.4 0.1 add_divide_fusion.3
  195.5 0.1 multiply_add_fusion
  195.7 9.4 %all_to_all.30 = bf16[16,32,75]{2,1,0:T(8,128)(2,1)S(1)} all-to-all(bf16[16,32,75]{2,1,0:T(8,128)(2,1)S(1)} %broadcast_in_dim.79), channel_id=1, replica_groups=mesh['task'=8,'tp'=16] {'tp'}, dimensions={0} | all-to-all | bytes 153600 | tf_op jit(solution)/shard_map/all_to_all | solution.py:17
  205.1 1.3 fusion.5
  206.4 3.3 convolution_convert_fusion
  209.7 67.1 %reduce-scatter.5.cloned.1.call-done = bf16[32,4096]{1,0:T(8,128)(2,1)} async-done(((bf16[512,4096]{1,0:T(8,128)(2,1)}), bf16[32,4096]{1,0:T(8,128)(2,1)}) %reduce-scatter.5.cloned.1.call-update) | async-done | bytes 262160 | tf_op jit(solution)/shard_map/reduce_scatter | solution.py:245
  276.8 1.8 fusion.13
  278.7 1.3 fusion.10
  279.9 2.5 stack.2
  282.4 7.2 %all-to-all-start.3 = ((bf16[16,32,4096]{2,1,0:T(8,128)(2,1)}), bf16[16,32,4096]{2,1,0:T(8,128)(2,1)}, u32[]{:S(2)}, u32[]{:S(2)}) async-start(bf16[16,32,4096]{2,1,0:T(8,128)(2,1)} %stack.2), calls=%async_computation.5 | async-start | bytes 8388608 | tf_op jit(solution)/shard_map/all_to_all | solution.py:258
  289.6 0.2 all-reduce.8.cloned.1.call-start
  289.8 4.8 convolution_convert_fusion.2
  294.7 44.6 %all-to-all-done.3 = bf16[16,32,4096]{2,1,0:T(8,128)(2,1)} async-done(((bf16[16,32,4096]{2,1,0:T(8,128)(2,1)}), bf16[16,32,4096]{2,1,0:T(8,128)(2,1)}, u32[]{:S(2)}, u32[]{:S(2)}) %all-to-all-start.3) | async-done | bytes 4194336 | tf_op jit(solution)/shard_map/all_to_all | solution.py:258
  339.2 4.8 convolution_convert_fusion.3
  344.0 9.4 %fusion.4 = bf16[4096,256]{0,1:T(8,128)(2,1)} fusion(bf16[512,4096]{1,0:T(8,128)(2,1)} %all-gather.4.cloned.1.call-done, bf16[512,4096]{1,0:T(8,128)(2,1)} %bitcast.19, bf16[256,4096]{1,0:T(8,128)(2,1)S(1)} %copy-done, f32[512,256]{1,0:T(8,128)S(1)} %fusion.46), kind=kOutput, calls=%fused_computation.11 | convolution fusion | flops 2149711872 | bytes 13107200 | tf_op jit(solution)/shard_map/dot_general | solution.py:265
  353.5 4.3 all-to-all-start.4
  357.7 0.2 convolution_convert_fusion.6
  357.9 0.1 reduce_sum.163
  358.0 5.5 %all-to-all-done.4 = f32[16,1,256]{2,1,0:T(1,128)S(1)} async-done(((f32[16,1,256]{2,1,0:T(1,128)}), f32[16,1,256]{2,1,0:T(1,128)S(1)}, u32[]{:S(2)}, u32[]{:S(2)}) %all-to-all-start.4) | async-done | bytes 16416 | tf_op jit(solution)/shard_map/all_to_all | solution.py:58
  363.6 38.7 %all-reduce.4 = (bf16[256]{0:T(256)(128)(2,1)S(1)}, bf16[256,75]{0,1:T(8,128)(2,1)S(1)}, bf16[75]{0:T(256)(128)(2,1)S(1)}) all-reduce(bf16[256]{0:T(256)(128)(2,1)S(1)} %reduce_sum.162, bf16[256,75]{0,1:T(8,128)(2,1)S(1)} %convolution_convert_fusion.6, bf16[75]{0:T(256)(128)(2,1)S(1)} %reduce_sum.163), channel_id=1, replica_groups=mesh['task'=8,'tp'=16] {'task'}, use_global_device_ids=true, to_apply=%region_23.24 | all-reduce | flops 19531 | bytes 78124 | tf_op jit(solution)/shard_map/psum | solution.py:270
  402.3 0.6 convert_element_type.138
  402.8 0.5 convert_element_type.141
  403.4 0.6 convert_element_type.140
  404.0 96.7 %all-reduce.8.cloned.1.call-done = (bf16[4096,256]{0,1:T(8,128)(2,1)}, bf16[256,4096]{1,0:T(8,128)(2,1)}, bf16[4096,256]{1,0:T(8,128)(2,1)}) async-done(((bf16[4096,256]{0,1:T(8,128)(2,1)}, bf16[256,4096]{1,0:T(8,128)(2,1)}, bf16[4096,256]{1,0:T(8,128)(2,1)}), (bf16[4096,256]{0,1:T(8,128)(2,1)}, bf16[256,4096]{1,0:T(8,128)(2,1)}, bf16[4096,256]{1,0:T(8,128)(2,1)})) %all-reduce.8.cloned.1.call-update) | async-done | bytes 6291472 | tf_op jit(solution)/shard_map/psum | solution.py:267
  500.7 4.3 copy.105
  505.0 4.2 convert_element_type.134
  509.2 2.3 convert_element_type.136
  (140 shorter events, 3.4 us)
Async XLA Ops:
  7.2 55.3 %copy-start = (bf16[256,4096]{1,0:T(8,128)(2,1)S(1)}, bf16[256,4096]{1,0:T(8,128)(2,1)}, u32[]{:S(2)}) copy-start(bf16[256,4096]{1,0:T(8,128)(2,1)} %param.21) | copy-start | bytes 6291460
  7.2 51.2 %all-gather.4.cloned.1.call-start = ((), (), s32[]{:S(2)}) async-start(), calls=%async_computation.7 | async-start | bytes 4456448 | tf_op jit(solution)/shard_map/all_gather | solution.py:191
  7.9 126.2 %reduce-scatter.3.cloned.1.call-start = ((), (), s32[]{:S(2)}) async-start(), calls=%async_computation.8 | async-start | bytes 4456448 | tf_op jit(solution)/shard_map/reduce_scatter | solution.py:199
  62.5 3.5 copy-start.17
  65.8 71.9 %copy-start.7 = (s32[32,15]{0,1:T(8,128)S(1)}, s32[32,15]{0,1:T(8,128)}, u32[]{:S(2)}) copy-start(s32[32,15]{0,1:T(8,128)} %param.30) | copy-start | bytes 5764
  65.8 72.1 %copy-start.6 = (f32[32,15]{0,1:T(8,128)S(1)}, f32[32,15]{0,1:T(8,128)}, u32[]{:S(2)}) copy-start(f32[32,15]{0,1:T(8,128)} %param.29) | copy-start | bytes 5764
  65.8 73.3 %copy-start.18 = (s32[32]{0:T(128)S(1)}, s32[32]{0:T(128)}, u32[]{:S(2)}) copy-start(s32[32]{0:T(128)} %param.27) | copy-start | bytes 388
  65.8 80.6 %copy-start.9 = (f32[32,15]{0,1:T(8,128)S(1)}, f32[32,15]{0,1:T(8,128)}, u32[]{:S(2)}) copy-start(f32[32,15]{0,1:T(8,128)} %param.31) | copy-start | bytes 5764
  65.8 80.7 %copy-start.8 = (s32[32,15]{0,1:T(8,128)S(1)}, s32[32,15]{0,1:T(8,128)}, u32[]{:S(2)}) copy-start(s32[32,15]{0,1:T(8,128)} %param.28) | copy-start | bytes 5764
  65.8 87.1 %copy-start.12 = (f32[57]{0:T(128)S(1)}, f32[57]{0:T(128)}, u32[]{:S(2)}) copy-start(f32[57]{0:T(128)} %param.25) | copy-start | bytes 688
  65.8 87.1 %copy-start.13 = (f32[57]{0:T(128)S(1)}, f32[57]{0:T(128)}, u32[]{:S(2)}) copy-start(f32[57]{0:T(128)} %param.26) | copy-start | bytes 688
  65.8 87.0 %copy-start.14 = (f32[75]{0:T(128)S(1)}, f32[75]{0:T(128)}, u32[]{:S(2)}) copy-start(f32[75]{0:T(128)} %param.24) | copy-start | bytes 904
  65.9 87.6 %copy-start.5 = (bf16[256,75]{0,1:T(8,128)(2,1)S(1)}, bf16[256,75]{0,1:T(8,128)(2,1)}, u32[]{:S(2)}) copy-start(bf16[256,75]{0,1:T(8,128)(2,1)} %param.23) | copy-start | bytes 115204
  65.9 111.0 %all-gather.6.cloned.1.call-start = ((), (), s32[]{:S(2)}) async-start(), calls=%async_computation.9 | async-start | bytes 4456448 | tf_op jit(solution)/shard_map/all_gather | solution.py:208
  135.8 1.9 copy-start.10
  140.1 12.7 %all-to-all-start = ((f32[8,1,171]{2,1,0:T(1,128)}), f32[8,1,171]{2,1,0:T(1,128)S(1)}, u32[]{:S(2)}, u32[]{:S(2)}) async-start(f32[8,1,171]{2,1,0:T(1,128)} %broadcast_in_dim.72), calls=%async_computation.1 | async-start | bytes 16384 | tf_op jit(solution)/shard_map/all_to_all | solution.py:17
  153.0 28.8 %copy-start.15 = (f32[57]{0:T(128)}, f32[57]{0:T(128)S(1)}, u32[]{:S(2)}) copy-start(f32[57]{0:T(128)S(1)} %get-tuple-element.394) | copy-start | bytes 688
  153.0 28.8 %copy-start.16 = (f32[57]{0:T(128)}, f32[57]{0:T(128)S(1)}, u32[]{:S(2)}) copy-start(f32[57]{0:T(128)S(1)} %get-tuple-element.395) | copy-start | bytes 688
  153.6 51.5 %copy-start.4 = (bf16[256,75]{0,1:T(8,128)(2,1)}, bf16[256,75]{0,1:T(8,128)(2,1)S(1)}, u32[]{:S(2)}) copy-start(bf16[256,75]{0,1:T(8,128)(2,1)S(1)} %multiply_convert_fusion.3) | copy-start | bytes 115204
  182.8 10.3 %all-to-all-start.1 = ((bf16[16,32,75]{2,1,0:T(8,128)(2,1)}), bf16[16,32,75]{2,1,0:T(8,128)(2,1)S(1)}, u32[]{:S(2)}, u32[]{:S(2)}) async-start(bf16[16,32,75]{2,1,0:T(8,128)(2,1)} %bitcast.8), calls=%async_computation.2 | async-start | bytes 262144 | tf_op jit(solution)/shard_map/all_to_all | solution.py:41
  186.9 89.9 %reduce-scatter.5.cloned.1.call-start = ((), (), s32[]{:S(2)}) async-start(), calls=%async_computation.10 | async-start | bytes 4456448 | tf_op jit(solution)/shard_map/reduce_scatter | solution.py:245
  187.0 6.0 %copy-start.11 = (f32[75]{0:T(128)}, f32[75]{0:T(128)S(1)}, u32[]{:S(2)}) copy-start(f32[75]{0:T(128)S(1)} %pad_maximum_fusion.1) | copy-start | bytes 904
  195.2 11.2 %copy-start.3 = (bf16[4096,256]{1,0:T(8,128)(2,1)S(1)}, bf16[4096,256]{1,0:T(8,128)(2,1)}, u32[]{:S(2)}) copy-start(bf16[4096,256]{1,0:T(8,128)(2,1)} %param.22) | copy-start | bytes 6291460
  209.7 67.1 %copy-start.1 = (bf16[32,4096]{1,0:T(8,128)(2,1)S(1)}, bf16[32,4096]{1,0:T(8,128)(2,1)}, u32[]{:S(2)}) copy-start(bf16[32,4096]{1,0:T(8,128)(2,1)} %reduce-scatter.3.cloned.1.call-done) | copy-start | bytes 786436
  282.4 56.8 %all-to-all-start.3 = ((bf16[16,32,4096]{2,1,0:T(8,128)(2,1)}), bf16[16,32,4096]{2,1,0:T(8,128)(2,1)}, u32[]{:S(2)}, u32[]{:S(2)}) async-start(bf16[16,32,4096]{2,1,0:T(8,128)(2,1)} %stack.2), calls=%async_computation.5 | async-start | bytes 8388608 | tf_op jit(solution)/shard_map/all_to_all | solution.py:258
  289.6 211.1 %all-reduce.8.cloned.1.call-start = ((), (), s32[]{:S(2)}) async-start(), calls=%async_computation.11 | async-start | bytes 12582912 | tf_op jit(solution)/shard_map/psum | solution.py:267
  353.5 10.1 %all-to-all-start.4 = ((f32[16,1,256]{2,1,0:T(1,128)}), f32[16,1,256]{2,1,0:T(1,128)S(1)}, u32[]{:S(2)}, u32[]{:S(2)}) async-start(f32[16,1,256]{2,1,0:T(1,128)} %bitcast.21), calls=%async_computation.6 | async-start | bytes 32768 | tf_op jit(solution)/shard_map/all_to_all | solution.py:58
  505.0 4.3 copy-start.2
Sparse Core Ops, SparseCore 0:
  9.6 48.6 all-gather.3
  66.0 68.0 reduce-scatter.2
  137.8 38.9 all-gather.5
  209.9 66.9 reduce-scatter.4
  353.6 147.0 all-reduce.7
